TPU v7x, 32 devices: a whole 2x2x4 slice. The times are simulated.
32 devices in a mesh: fsdp: 4 (over y, core), tp: 4 (over z), rollout: 2 (over x).
Axes of the slice: x: 2, y: 2, z: 4, core: 2. Of those that a mesh axis runs over, the one named last changes fastest.
Arguments:
- weights: bfloat16 [2, 4096, 14336], P('rollout', 'fsdp', 'tp'), may hold values from -6 to 6
- gradient: bfloat16 [2, 4096, 14336], P('rollout', 'fsdp', 'tp'), may hold values from -6 to 6
- momentum: float32 [2, 4096, 14336], P('rollout', 'fsdp', 'tp'), may hold values from -90 to 90
- basis: float32 [2, 14336, 512], P('rollout', 'tp'), may hold values from -6 to 6
Outputs:
- weights_next: bfloat16 [2, 4096, 14336], P('rollout', 'fsdp', 'tp')
- momentum_next: float32 [2, 4096, 14336], P('rollout', 'fsdp', 'tp')
- basis_next: float32 [2, 14336, 512], P('rollout', 'tp')
- rollout_weights: bfloat16 [2, 4096, 14336], P(None, 'fsdp', 'tp')
All inputs are finite; a program needn't handle non-finite values.
Results may differ from a plain program's by a relative error of at most 0.013.
Values may be sent and summed in bfloat16 or wider, within the bound.
A program may use at most 192 MiB of HBM per device.

v0:
```python
import jax
import jax.numpy as jnp
from jax import lax
from jax.sharding import PartitionSpec as P

COLS = 14336
HIGH = lax.Precision.HIGHEST


def body(weights, gradient, momentum, basis):
    blend = momentum[0] + gradient[0].astype(jnp.float32)
    prior = basis[0]
    share = lax.psum_scatter(
        jnp.dot(blend, prior, precision=HIGH, preferred_element_type=jnp.float32),
        "tp",
        scatter_dimension=0,
        tiled=True,
    )
    gram = lax.psum(
        jnp.dot(share.T, share, precision=HIGH, preferred_element_type=jnp.float32), ("fsdp", "tp")
    )
    left = lax.all_gather(share, "tp", axis=0, tiled=True)
    lower = jnp.linalg.cholesky(gram)
    ortho = lax.linalg.triangular_solve(lower, left, left_side=False, lower=True, transpose_a=True)
    partial_right = jnp.dot(blend.T, ortho, precision=HIGH, preferred_element_type=jnp.float32)
    right = lax.psum(partial_right.astype(jnp.bfloat16), "fsdp").astype(jnp.float32)
    squares = lax.psum(jnp.sum(right * right, axis=0), "tp")
    meansq = squares / COLS
    basis_new = right * lax.rsqrt(meansq + 1e-06)
    norms = jnp.sqrt(meansq + 1e-06)
    moment_new = blend - 0.05 * jnp.dot(
        ortho * norms, basis_new.T, precision=HIGH, preferred_element_type=jnp.float32
    )
    update = jnp.dot(ortho, basis_new.T, precision=HIGH, preferred_element_type=jnp.float32)
    weight_new = (weights[0].astype(jnp.float32) - 0.3 * update).astype(jnp.bfloat16)[None]
    rollout_copy = lax.all_gather(weight_new, "rollout", axis=0, tiled=True)
    return (weight_new, moment_new[None], basis_new[None], rollout_copy)


def solution(mesh):
    return jax.shard_map(
        body,
        mesh=mesh,
        in_specs=(
            P("rollout", "fsdp", "tp"),
            P("rollout", "fsdp", "tp"),
            P("rollout", "fsdp", "tp"),
            P("rollout", "tp", None),
        ),
        out_specs=(
            P("rollout", "fsdp", "tp"),
            P("rollout", "fsdp", "tp"),
            P("rollout", "tp", None),
            P(None, "fsdp", "tp"),
        ),
        check_vma=False,
    )
```

profile of v0, /device:TPU:0, one launch (start us, length us, event | category | flops | bytes accessed | tf_op | source)
XLA Modules:
  0.0 710.0 jit_solution(7459058599054322177)
XLA Ops:
  7.2 29.3 %fusion.3 = f32[1024,512]{1,0:T(8,128)} fusion(f32[1,3584,512]{2,1,0:T(8,128)} %param.7, f32[1,1024,3584]{2,1,0:T(8,128)} %param.6, bf16[1,1024,3584]{2,1,0:T(8,128)(2,1)} %param.5), kind=kOutput, calls=%fused_computation.7 | convolution fusion | flops 22555918336 | bytes 31457280 | tf_op jit(solution)/shard_map/dot_general | solution.py:14
  36.5 46.5 %reduce-scatter.2.cloned.1.call-done = f32[256,512]{1,0:T(8,128)} async-done(((f32[1024,512]{1,0:T(8,128)}), f32[256,512]{1,0:T(8,128)}) %reduce-scatter.2.cloned.1.call-update) | async-done | bytes 524304 | tf_op jit(solution)/shard_map/reduce_scatter | solution.py:13
  83.0 3.2 fusion.58
  86.3 0.7 all-gather.4.cloned.1.call-update
  87.0 0.5 all-reduce.6.cloned.1.call-start
  87.5 92.5 %all-reduce.4.cloned.1.call-done = f32[512,512]{0,1:T(8,128)} async-done(((f32[512,512]{0,1:T(8,128)}), f32[512,512]{0,1:T(8,128)}) %all-reduce.4.cloned.1.call-update) | async-done | bytes 1048592 | tf_op jit(solution)/shard_map/psum | solution.py:19
  180.0 1.6 copy.9
  181.6 1.4 fusion.29
  183.1 11.7 %cholesky.104 = f32[128,128]{1,0:T(8,128)S(1)} custom-call(f32[128,128]{1,0:T(8,128)S(1)} %cholesky.266), custom_call_target="Cholesky" | custom-call | tf_op jit(solution)/shard_map/jit(cholesky)/cholesky | solution.py:23
  194.8 9.8 %custom-call.30 = f32[1,128,128]{1,2,0:T(8,128)S(1)} custom-call(f32[1,128,128]{2,1,0:T(8,128)S(1)} %get-tuple-element.31), custom_call_target="InvertDiagBlocksLowerTriangular" | custom-call | tf_op jit(solution)/shard_map/jit(cholesky)/cholesky | solution.py:23
  204.8 0.3 constant_dynamic-update-slice_fusion.3
  205.1 0.3 convolution_subtract_fusion.2
  205.4 11.7 %cholesky.217 = f32[128,128]{1,0:T(8,128)S(1)} custom-call(f32[128,128]{1,0:T(8,128)S(1)} %cholesky.270), custom_call_target="Cholesky" | custom-call | tf_op jit(solution)/shard_map/jit(cholesky)/cholesky | solution.py:23
  217.2 10.0 %custom-call.31 = f32[1,128,128]{1,2,0:T(8,128)S(1)} custom-call(f32[1,128,128]{2,1,0:T(8,128)S(1)} %get-tuple-element.28), custom_call_target="InvertDiagBlocksLowerTriangular" | custom-call | tf_op jit(solution)/shard_map/jit(cholesky)/cholesky | solution.py:23
  227.4 0.4 convolution_subtract_fusion.3
  227.8 11.7 %cholesky.238 = f32[128,128]{1,0:T(8,128)S(1)} custom-call(f32[128,128]{1,0:T(8,128)S(1)} %cholesky.275), custom_call_target="Cholesky" | custom-call | tf_op jit(solution)/shard_map/jit(cholesky)/cholesky | solution.py:23
  239.6 9.8 %custom-call.32 = f32[1,128,128]{1,2,0:T(8,128)S(1)} custom-call(f32[1,128,128]{2,1,0:T(8,128)S(1)} %get-tuple-element.25), custom_call_target="InvertDiagBlocksLowerTriangular" | custom-call | tf_op jit(solution)/shard_map/jit(cholesky)/cholesky | solution.py:23
  249.6 0.4 convolution_subtract_fusion.4
  250.0 11.7 %cholesky.255 = f32[128,128]{1,0:T(8,128)S(1)} custom-call(f32[128,128]{1,0:T(8,128)S(1)} %convolution_subtract_fusion.4), custom_call_target="Cholesky" | custom-call | tf_op jit(solution)/shard_map/jit(cholesky)/cholesky | solution.py:23
  261.7 0.6 compare_reduce_fusion.2
  263.6 0.6 compare_reduce_fusion.1
  265.0 0.6 compare_reduce_fusion
  266.6 8.0 %while.1 = (s32[]{:T(128)}, f32[512,512]{1,0:T(8,128)S(1)}, s32[4,2]{0,1:T(2,128)S(1)}, f32[4,128,128]{2,1,0:T(8,128)S(1)}, s32[]{:T(128)}) while((s32[]{:T(128)}, f32[512,512]{1,0:T(8,128)S(1)}, s32[4,2]{0,1:T(2,128)S(1)}, f32[4,128,128]{2,1,0:T(8,128)S(1)}, s32[]{:T(128)}) %tuple.32), condition=%wide.while_cond, body=%wide.while_body.sunk | while | flops 2 | bytes 131189 | solution.py:24
  266.7 0.5 fusion.67
  267.2 1.4 bitcast_dynamic-update-slice_fusion.2
  268.7 0.5 fusion.67
  269.2 1.4 bitcast_dynamic-update-slice_fusion.2
  270.7 0.5 fusion.67
  271.2 1.4 bitcast_dynamic-update-slice_fusion.2
  272.7 0.5 fusion.67
  273.2 1.4 bitcast_dynamic-update-slice_fusion.2
  274.6 39.3 %custom-call.33 = f32[4,128,128]{1,2,0:T(8,128)S(1)} custom-call(f32[4,128,128]{2,1,0:T(8,128)S(1)} %get-tuple-element.11), custom_call_target="InvertDiagBlocksLowerTriangular" | custom-call | tf_op jit(solution)/shard_map/triangular_solve | solution.py:24
  314.0 1.7 fusion.31
  315.6 2.0 convolution_subtract_fusion.1
  317.7 0.6 fusion.43
  318.3 2.9 convolution_subtract_fusion
  321.2 0.6 fusion.42
  321.8 3.7 fusion.23
  325.5 0.6 fusion.41
  326.1 50.1 %fusion.11 = bf16[3584,512]{1,0:T(8,128)(2,1)} fusion(f32[1,1024,3584]{2,1,0:T(8,128)} %param.6, bf16[1,1024,3584]{2,1,0:T(8,128)(2,1)} %param.5, f32[1024,128]{0,1:T(8,128)S(1)} %fusion.41, f32[1024,128]{0,1:T(8,128)S(1)} %fusion.42, f32[1024,128]{0,1:T(8,128)S(1)} %fusion.43, f32[1024,128]{0,1:T(8,128)S(1)} %fusion.31), kind=kOutput, calls=%fused_computation.18 | convolution fusion | flops 22559326208 | bytes 27787264 | tf_op jit(solution)/shard_map/dot_general | solution.py:25
  376.3 76.2 %all-reduce.6.cloned.1.call-done = bf16[3584,512]{1,0:T(8,128)(2,1)} async-done(((bf16[3584,512]{1,0:T(8,128)(2,1)}), bf16[3584,512]{1,0:T(8,128)(2,1)}) %all-reduce.6.cloned.1.call-update) | async-done | bytes 3670032 | tf_op jit(solution)/shard_map/psum | solution.py:26
  452.5 2.9 fusion.9
  455.3 11.9 %psum.23 = f32[512]{0:T(512)S(1)} all-reduce(f32[512]{0:T(512)S(1)} %fusion.9), channel_id=1, replica_groups=mesh['fsdp'=4,'tp'=4,'rollout'=2] {'tp'}, use_global_device_ids=true, to_apply=%region_12.13 | all-reduce | flops 512 | bytes 4096 | tf_op jit(solution)/shard_map/psum | solution.py:27
  467.2 49.9 %fusion = bf16[1024,3584]{1,0:T(8,128)(2,1)} fusion(bf16[1,1024,3584]{2,1,0:T(8,128)(2,1)} %param.4, bf16[3584,512]{1,0:T(8,128)(2,1)} %all-reduce.6.cloned.1.call-done, f32[512]{0:T(512)S(1)} %get-tuple-element.33, f32[1024,128]{0,1:T(8,128)S(1)} %fusion.41, f32[1024,128]{0,1:T(8,128)S(1)} %fusion.42, f32[1024,128]{0,1:T(8,128)S(1)} %fusion.43, ...), kind=kOutput, calls=%fused_computation.3 | convolution fusion | flops 22568501248 | bytes 20449280 | tf_op jit(solution)/shard_map/dot_general | solution.py:34
  517.1 7.9 %fusion.6 = f32[1,3584,512]{2,1,0:T(8,128)} fusion(bf16[3584,512]{1,0:T(8,128)(2,1)} %all-reduce.6.cloned.1.call-done, f32[512]{0:T(512)S(1)} %get-tuple-element.33), kind=kLoop, calls=%fused_computation.13 | loop fusion | flops 3670016 | bytes 11012096 | tf_op jit(solution)/shard_map/broadcast_in_dim | solution.py:37
  525.0 52.9 %fusion.5 = f32[1,1024,3584]{2,1,0:T(8,128)} fusion(bf16[3584,512]{1,0:T(8,128)(2,1)S(1)} %copy-done, f32[1,1024,3584]{2,1,0:T(8,128)} %param.6, bf16[1,1024,3584]{2,1,0:T(8,128)(2,1)} %param.5, f32[512]{0:T(512)S(1)} %get-tuple-element.33, f32[512]{0:T(512)S(1)} %get-tuple-element.32, f32[1024,128]{0,1:T(8,128)S(1)} %fusion.41, ...), kind=kOutput, calls=%fused_computation.9 | convolution fusion | flops 22569025536 | bytes 42471424 | tf_op jit(solution)/shard_map/dot_general | solution.py:31
  577.9 112.2 %all-gather.6.cloned.1.call-done = bf16[2048,3584]{1,0:T(8,128)(2,1)} async-done(((bf16[1024,3584]{1,0:T(8,128)(2,1)}), bf16[2048,3584]{1,0:T(8,128)(2,1)}) %all-gather.6.cloned.1.call-update) | async-done | bytes 14680080 | tf_op jit(solution)/shard_map/all_gather | solution.py:36
  690.1 13.1 %copy.29 = bf16[2,1024,3584]{2,1,0:T(8,128)(2,1)} copy(bf16[2,1024,3584]{2,1,0:T(8,128)(2,1)} %bitcast.72) | data formatting | bytes 29360128
  (30 shorter events, 1.7 us)
Async XLA Ops:
  7.2 75.8 %reduce-scatter.2.cloned.1.call-start = ((), (), s32[]{:S(2)}) async-start(), calls=%async_computation.1 | async-start | bytes 2621440 | tf_op jit(solution)/shard_map/reduce_scatter | solution.py:13
  36.5 143.6 %all-reduce.4.cloned.1.call-start = ((), (), s32[]{:S(2)}) async-start(), calls=%async_computation.3 | async-start | bytes 2097152 | tf_op jit(solution)/shard_map/psum | solution.py:19
  86.2 227.7 %all-gather.4.cloned.1.call-start = ((), (), s32[]{:S(2)}) async-start(), calls=%async_computation.2 | async-start | bytes 2621440 | tf_op jit(solution)/shard_map/all_gather | solution.py:22
  87.0 365.5 %all-reduce.6.cloned.1.call-start = ((), (), s32[]{:S(2)}) async-start(), calls=%async_computation.4 | async-start | bytes 7340032 | tf_op jit(solution)/shard_map/psum | solution.py:26
  376.2 313.9 %all-gather.6.cloned.1.call-start = ((), (), s32[]{:S(2)}) async-start(), calls=%async_computation.5 | async-start | bytes 22020096 | tf_op jit(solution)/shard_map/all_gather | solution.py:36
  517.1 7.9 %copy-start = (bf16[3584,512]{1,0:T(8,128)(2,1)S(1)}, bf16[3584,512]{1,0:T(8,128)(2,1)}, u32[]{:S(2)}) copy-start(bf16[3584,512]{1,0:T(8,128)(2,1)} %all-reduce.6.cloned.1.call-done) | copy-start | bytes 11010052
Sparse Core Ops, SparseCore 0:
  36.6 46.3 reduce-scatter.1
  87.0 92.9 all-reduce.3
  181.6 44.7 all-gather.3
  376.4 76.0 all-reduce.5
  517.2 172.8 all-gather.5
where the time goes:
time: 716 us; the launch traced here: 710 us
  waiting for transfers between devices  328 us (46%)
  matrix products  199 us (28%)
  other arithmetic  130 us (18%)
  local copies, waits for them, and re-layouts  22.9 us (3%)
  between operations  16.8 us (2%)
  blocking collectives  11.9 us (2%)
    all_gather x1, waiting for transfers between devices, body(): rollout_copy = lax.all_gather(weight_new, 'rollout', axis=0, tiled=True)  112 us
    psum x1, waiting for transfers between devices, body(): lax.psum(jnp.dot(share.T, share, precision=HIGH, preferred_element_type=j...  92.5 us
    another operation x14, other arithmetic, body(): lower = jnp.linalg.cholesky(gram)  78.5 us
    psum x1, waiting for transfers between devices, body(): lax.psum(partial_right.astype(jnp.bfloat16), 'fsdp').astype(jnp.float32)  76.2 us
    dot_general x1, matrix products, body(): jnp.dot(ortho * norms, basis_new.T, precision=HIGH, preferred_element_typ...  52.9 us
    dot_general x1, matrix products, body(): jnp.dot(blend.T, ortho, precision=HIGH, preferred_element_type=jnp.float32)  50.1 us
    dot_general x1, matrix products, body(): jnp.dot(ortho, basis_new.T, precision=HIGH, preferred_element_type=jnp.fl...  49.9 us
    reduce_scatter x1, waiting for transfers between devices, body(): lax.psum_scatter(jnp.dot(blend, prior, precision=HIGH, preferred_element_...  46.5 us
  transfers between devices with their start and end apart: 5, of which 4 were waited for; matrix products, arithmetic and copies ran while one was open for 27% of the time, Pallas kernels for 0%

commit v1 on v0

--- a/solution.py
+++ b/solution.py
@@ -16,9 +16,8 @@
         scatter_dimension=0,
         tiled=True,
     )
-    gram = lax.psum(
-        jnp.dot(share.T, share, precision=HIGH, preferred_element_type=jnp.float32), ("fsdp", "tp")
-    )
+    u = jnp.dot(share.T, share, precision=HIGH, preferred_element_type=jnp.float32)
+    gram = lax.all_gather(u, ("fsdp", "tp")).sum(axis=0)
     left = lax.all_gather(share, "tp", axis=0, tiled=True)
     lower = jnp.linalg.cholesky(gram)
     ortho = lax.linalg.triangular_solve(lower, left, left_side=False, lower=True, transpose_a=True)

time: 716 us -> 752 us (1.050)
  waiting for transfers between devices: 328 us -> 359 us
    all_gather x0 -> x1, waiting for transfers between devices: none -> 125 us  [body(): gram = lax.all_gather(u, ('fsdp', 'tp')).sum(axis=0)]
    psum x1 -> x0, waiting for transfers between devices: 92.5 us -> none  [body(): lax.psum(jnp.dot(share.T, share, precision=HIGH, preferred_element_type=j...]
    reduce_sum x0 -> x1, other arithmetic: none -> 7.91 us  [body(): gram = lax.all_gather(u, ('fsdp', 'tp')).sum(axis=0)]
  transfers between devices with their start and end apart: 5 -> 5, of which waited for: 4 -> 4; matrix products, arithmetic and copies ran while one was open for 27% -> 26% of each run, Pallas kernels for 0% -> 0%
where the time goes in v1:
time: 752 us; the launch traced here: 747 us
  waiting for transfers between devices  359 us (48%)
  matrix products  199 us (26%)
  other arithmetic  137 us (18%)
  local copies, waits for them, and re-layouts  21.5 us (3%)
  between operations  16.8 us (2%)
  blocking collectives  11.9 us (2%)
    all_gather x1, waiting for transfers between devices, body(): gram = lax.all_gather(u, ('fsdp', 'tp')).sum(axis=0)  125 us
    all_gather x1, waiting for transfers between devices, body(): rollout_copy = lax.all_gather(weight_new, 'rollout', axis=0, tiled=True)  112 us
    another operation x14, other arithmetic, body(): lower = jnp.linalg.cholesky(gram)  78.9 us
    psum x1, waiting for transfers between devices, body(): lax.psum(partial_right.astype(jnp.bfloat16), 'fsdp').astype(jnp.float32)  75.2 us
    dot_general x1, matrix products, body(): jnp.dot(ortho * norms, basis_new.T, precision=HIGH, preferred_element_typ...  52.9 us
    dot_general x1, matrix products, body(): jnp.dot(blend.T, ortho, precision=HIGH, preferred_element_type=jnp.float32)  50.1 us
    dot_general x1, matrix products, body(): jnp.dot(ortho, basis_new.T, precision=HIGH, preferred_element_type=jnp.fl...  49.9 us
    reduce_scatter x1, waiting for transfers between devices, body(): lax.psum_scatter(jnp.dot(blend, prior, precision=HIGH, preferred_element_...  46.5 us
  transfers between devices with their start and end apart: 5, of which 4 were waited for; matrix products, arithmetic and copies ran while one was open for 26% of the time, Pallas kernels for 0%

profile of v1, /device:TPU:0, one launch (start us, length us, event | category | flops | bytes accessed | tf_op | source)
XLA Modules:
  0.0 746.7 jit_solution(12389121948933850193)
XLA Ops:
  7.2 29.3 %fusion.3 = f32[1024,512]{1,0:T(8,128)} fusion(f32[1,3584,512]{2,1,0:T(8,128)} %param.7, f32[1,1024,3584]{2,1,0:T(8,128)} %param.6, bf16[1,1024,3584]{2,1,0:T(8,128)(2,1)} %param.5), kind=kOutput, calls=%fused_computation.7 | convolution fusion | flops 22555918336 | bytes 31457280 | tf_op jit(solution)/shard_map/dot_general | solution.py:14
  36.5 46.5 %reduce-scatter.2.cloned.1.call-done = f32[256,512]{1,0:T(8,128)} async-done(((f32[1024,512]{1,0:T(8,128)}), f32[256,512]{1,0:T(8,128)}) %reduce-scatter.2.cloned.1.call-update) | async-done | bytes 524304 | tf_op jit(solution)/shard_map/reduce_scatter | solution.py:13
  83.0 3.2 fusion.58
  86.3 0.7 all-gather.6.cloned.1.call-update
  87.2 124.8 %all-gather.8.cloned.1.call-done = f32[8192,512]{1,0:T(8,128)} async-done(((f32[512,512]{1,0:T(8,128)}), f32[8192,512]{1,0:T(8,128)}) %all-gather.8.cloned.1.call-update) | async-done | bytes 16777232 | tf_op jit(solution)/shard_map/all_gather | solution.py:20
  212.0 7.9 %reduce_sum.18 = f32[512,512]{1,0:T(8,128)S(1)} reduce(f32[16,512,512]{2,1,0:T(8,128)} %bitcast.73, f32[]{:T(128)} %constant.141.clone.1), dimensions={0}, to_apply=%region_1.0 | reduce | flops 3932160 | bytes 17825796 | tf_op jit(solution)/shard_map/reduce_sum | solution.py:20
  219.9 0.3 copy.9
  220.5 11.7 %cholesky.104 = f32[128,128]{1,0:T(8,128)S(1)} custom-call(f32[128,128]{1,0:T(8,128)S(1)} %cholesky.266), custom_call_target="Cholesky" | custom-call | tf_op jit(solution)/shard_map/jit(cholesky)/cholesky | solution.py:22
  232.4 9.8 %custom-call.30 = f32[1,128,128]{1,2,0:T(8,128)S(1)} custom-call(f32[1,128,128]{2,1,0:T(8,128)S(1)} %get-tuple-element.31), custom_call_target="InvertDiagBlocksLowerTriangular" | custom-call | tf_op jit(solution)/shard_map/jit(cholesky)/cholesky | solution.py:22
  242.2 0.3 constant_dynamic-update-slice_fusion.3
  242.5 0.3 convolution_subtract_fusion.2
  242.9 12.1 %cholesky.217 = f32[128,128]{1,0:T(8,128)S(1)} custom-call(f32[128,128]{1,0:T(8,128)S(1)} %cholesky.270), custom_call_target="Cholesky" | custom-call | tf_op jit(solution)/shard_map/jit(cholesky)/cholesky | solution.py:22
  255.0 9.8 %custom-call.31 = f32[1,128,128]{1,2,0:T(8,128)S(1)} custom-call(f32[1,128,128]{2,1,0:T(8,128)S(1)} %get-tuple-element.28), custom_call_target="InvertDiagBlocksLowerTriangular" | custom-call | tf_op jit(solution)/shard_map/jit(cholesky)/cholesky | solution.py:22
  264.8 0.3 convolution_dynamic-update-slice_fusion
  265.1 0.4 convolution_subtract_fusion.3
  265.5 11.7 %cholesky.238 = f32[128,128]{1,0:T(8,128)S(1)} custom-call(f32[128,128]{1,0:T(8,128)S(1)} %cholesky.275), custom_call_target="Cholesky" | custom-call | tf_op jit(solution)/shard_map/jit(cholesky)/cholesky | solution.py:22
  277.2 9.8 %custom-call.32 = f32[1,128,128]{1,2,0:T(8,128)S(1)} custom-call(f32[1,128,128]{2,1,0:T(8,128)S(1)} %get-tuple-element.25), custom_call_target="InvertDiagBlocksLowerTriangular" | custom-call | tf_op jit(solution)/shard_map/jit(cholesky)/cholesky | solution.py:22
  287.3 0.4 convolution_subtract_fusion.4
  287.7 11.9 %cholesky.255 = f32[128,128]{1,0:T(8,128)S(1)} custom-call(f32[128,128]{1,0:T(8,128)S(1)} %convolution_subtract_fusion.4), custom_call_target="Cholesky" | custom-call | tf_op jit(solution)/shard_map/jit(cholesky)/cholesky | solution.py:22
  299.5 0.6 compare_reduce_fusion.2
  301.5 0.6 compare_reduce_fusion.1
  302.8 0.6 compare_reduce_fusion
  304.2 8.0 %while.1 = (s32[]{:T(128)}, f32[512,512]{1,0:T(8,128)S(1)}, s32[4,2]{0,1:T(2,128)S(1)}, f32[4,128,128]{2,1,0:T(8,128)S(1)}, s32[]{:T(128)}) while((s32[]{:T(128)}, f32[512,512]{1,0:T(8,128)S(1)}, s32[4,2]{0,1:T(2,128)S(1)}, f32[4,128,128]{2,1,0:T(8,128)S(1)}, s32[]{:T(128)}) %tuple.32), condition=%wide.while_cond, body=%wide.while_body.sunk | while | flops 2 | bytes 131189 | solution.py:23
  304.3 0.5 fusion.67
  304.8 1.4 bitcast_dynamic-update-slice_fusion.2
  306.3 0.5 fusion.67
  306.8 1.4 bitcast_dynamic-update-slice_fusion.2
  308.3 0.5 fusion.67
  308.9 1.4 bitcast_dynamic-update-slice_fusion.2
  310.3 0.5 fusion.67
  310.9 1.4 bitcast_dynamic-update-slice_fusion.2
  312.3 39.3 %custom-call.33 = f32[4,128,128]{1,2,0:T(8,128)S(1)} custom-call(f32[4,128,128]{2,1,0:T(8,128)S(1)} %get-tuple-element.11), custom_call_target="InvertDiagBlocksLowerTriangular" | custom-call | tf_op jit(solution)/shard_map/triangular_solve | solution.py:23
  351.6 1.7 fusion.31
  353.3 2.0 convolution_subtract_fusion.1
  355.3 0.6 fusion.43
  355.9 2.9 convolution_subtract_fusion
  358.8 0.6 fusion.42
  359.4 3.7 fusion.23
  363.1 0.6 fusion.41
  363.8 50.1 %fusion.11 = bf16[3584,512]{1,0:T(8,128)(2,1)} fusion(f32[1,1024,3584]{2,1,0:T(8,128)} %param.6, bf16[1,1024,3584]{2,1,0:T(8,128)(2,1)} %param.5, f32[1024,128]{0,1:T(8,128)S(1)} %fusion.41, f32[1024,128]{0,1:T(8,128)S(1)} %fusion.42, f32[1024,128]{0,1:T(8,128)S(1)} %fusion.43, f32[1024,128]{0,1:T(8,128)S(1)} %fusion.31), kind=kOutput, calls=%fused_computation.18 | convolution fusion | flops 22559326208 | bytes 27787264 | tf_op jit(solution)/shard_map/dot_general | solution.py:24
  413.9 75.2 %all-reduce.3.cloned.1.call-done = bf16[3584,512]{1,0:T(8,128)(2,1)} async-done(((bf16[3584,512]{1,0:T(8,128)(2,1)}), bf16[3584,512]{1,0:T(8,128)(2,1)}) %all-reduce.3.cloned.1.call-update) | async-done | bytes 3670032 | tf_op jit(solution)/shard_map/psum | solution.py:25
  489.2 2.9 fusion.9
  492.1 11.9 %psum.15 = f32[512]{0:T(512)S(1)} all-reduce(f32[512]{0:T(512)S(1)} %fusion.9), channel_id=1, replica_groups=mesh['fsdp'=4,'tp'=4,'rollout'=2] {'tp'}, use_global_device_ids=true, to_apply=%region_12.13 | all-reduce | flops 512 | bytes 4096 | tf_op jit(solution)/shard_map/psum | solution.py:26
  503.9 49.9 %fusion = bf16[1024,3584]{1,0:T(8,128)(2,1)} fusion(bf16[1,1024,3584]{2,1,0:T(8,128)(2,1)} %param.4, bf16[3584,512]{1,0:T(8,128)(2,1)} %all-reduce.3.cloned.1.call-done, f32[512]{0:T(512)S(1)} %get-tuple-element.33, f32[1024,128]{0,1:T(8,128)S(1)} %fusion.41, f32[1024,128]{0,1:T(8,128)S(1)} %fusion.42, f32[1024,128]{0,1:T(8,128)S(1)} %fusion.43, ...), kind=kOutput, calls=%fused_computation.3 | convolution fusion | flops 22568501248 | bytes 20449280 | tf_op jit(solution)/shard_map/dot_general | solution.py:33
  553.8 7.9 %fusion.6 = f32[1,3584,512]{2,1,0:T(8,128)} fusion(bf16[3584,512]{1,0:T(8,128)(2,1)} %all-reduce.3.cloned.1.call-done, f32[512]{0:T(512)S(1)} %get-tuple-element.33), kind=kLoop, calls=%fused_computation.13 | loop fusion | flops 3670016 | bytes 11012096 | tf_op jit(solution)/shard_map/broadcast_in_dim | solution.py:36
  561.7 52.9 %fusion.5 = f32[1,1024,3584]{2,1,0:T(8,128)} fusion(bf16[3584,512]{1,0:T(8,128)(2,1)S(1)} %copy-done, f32[1,1024,3584]{2,1,0:T(8,128)} %param.6, bf16[1,1024,3584]{2,1,0:T(8,128)(2,1)} %param.5, f32[512]{0:T(512)S(1)} %get-tuple-element.33, f32[512]{0:T(512)S(1)} %get-tuple-element.32, f32[1024,128]{0,1:T(8,128)S(1)} %fusion.41, ...), kind=kOutput, calls=%fused_computation.9 | convolution fusion | flops 22569025536 | bytes 42471424 | tf_op jit(solution)/shard_map/dot_general | solution.py:30
  614.6 112.2 %all-gather.10.cloned.1.call-done = bf16[2048,3584]{1,0:T(8,128)(2,1)} async-done(((bf16[1024,3584]{1,0:T(8,128)(2,1)}), bf16[2048,3584]{1,0:T(8,128)(2,1)}) %all-gather.10.cloned.1.call-update) | async-done | bytes 14680080 | tf_op jit(solution)/shard_map/all_gather | solution.py:35
  726.8 13.1 %copy.27 = bf16[2,1024,3584]{2,1,0:T(8,128)(2,1)} copy(bf16[2,1024,3584]{2,1,0:T(8,128)(2,1)} %bitcast.74) | data formatting | bytes 29360128
  (31 shorter events, 1.6 us)
Async XLA Ops:
  7.2 75.8 %reduce-scatter.2.cloned.1.call-start = ((), (), s32[]{:S(2)}) async-start(), calls=%async_computation.1 | async-start | bytes 2621440 | tf_op jit(solution)/shard_map/reduce_scatter | solution.py:13
  36.5 175.5 %all-gather.8.cloned.1.call-start = ((), (), s32[]{:S(2)}) async-start(), calls=%async_computation.4 | async-start | bytes 17825792 | tf_op jit(solution)/shard_map/all_gather | solution.py:20
  86.2 265.4 %all-gather.6.cloned.1.call-start = ((), (), s32[]{:S(2)}) async-start(), calls=%async_computation.2 | async-start | bytes 2621440 | tf_op jit(solution)/shard_map/all_gather | solution.py:21
  87.0 402.2 %all-reduce.3.cloned.1.call-start = ((), (), s32[]{:S(2)}) async-start(), calls=%async_computation.3 | async-start | bytes 7340032 | tf_op jit(solution)/shard_map/psum | solution.py:25
  413.9 312.9 %all-gather.10.cloned.1.call-start = ((), (), s32[]{:S(2)}) async-start(), calls=%async_computation.5 | async-start | bytes 22020096 | tf_op jit(solution)/shard_map/all_gather | solution.py:35
  553.8 7.9 %copy-start = (bf16[3584,512]{1,0:T(8,128)(2,1)S(1)}, bf16[3584,512]{1,0:T(8,128)(2,1)}, u32[]{:S(2)}) copy-start(bf16[3584,512]{1,0:T(8,128)(2,1)} %all-reduce.3.cloned.1.call-done) | copy-start | bytes 11010052
Sparse Core Ops, SparseCore 0:
  36.6 46.3 reduce-scatter.1
  86.3 125.6 all-gather.7
  213.6 43.9 all-gather.5
  414.0 75.1 all-reduce.2
  553.9 172.8 all-gather.9
